TPU v7x, 32 devices: a whole 2x2x4 slice. The times are simulated.
32 devices in a mesh: lat: 4 (over z), lon: 8 (over y, x, core).
Axes of the slice: x: 2, y: 2, z: 4, core: 2. Of those that a mesh axis runs over, the one named last changes fastest.
Arguments:
- grid_latent: bfloat16 [16384, 512], P(('lat', 'lon')), may hold values from -6 to 6
- mesh_latent: bfloat16 [4096, 512], P(('lat', 'lon')), may hold values from -6 to 6
- block_weights: bfloat16 [4, 3, 512, 512], replicated, may hold values from -0.25 to 0.25
- block_gains: float32 [4, 512], replicated, may hold values from 0.5 to 1.5
- grid_cot: bfloat16 [16384, 512], P(('lat', 'lon')), may hold values from -0.046875 to 0.046875
- encode_rows: int32 [32, 32, 4], P(('lat', 'lon')), may hold values from 0 to 511
- encode_senders: int32 [32, 1536], P(('lat', 'lon')), may hold values from 0 to 127, as said below
- encode_receivers: int32 [32, 1536], P(('lat', 'lon')), may hold values from 0 to 127, as said below
- encode_blocks: int32 [32], P(('lat', 'lon')), may hold values from 4 to 12, as said below
- process_rows: int32 [32, 32, 4], P(('lat', 'lon')), may hold values from 0 to 127
- process_senders: int32 [32, 1536], P(('lat', 'lon')), may hold values from 0 to 127, as said below
- process_receivers: int32 [32, 1536], P(('lat', 'lon')), may hold values from 0 to 127, as said below
- process_blocks: int32 [32], P(('lat', 'lon')), may hold values from 4 to 12, as said below
- decode_rows: int32 [32, 32, 4], P(('lat', 'lon')), may hold values from 0 to 127
- decode_senders: int32 [32, 1536], P(('lat', 'lon')), may hold values from 0 to 127, as said below
- decode_receivers: int32 [32, 1536], P(('lat', 'lon')), may hold values from 0 to 511, as said below
- decode_blocks: int32 [32], P(('lat', 'lon')), may hold values from 4 to 12, as said below
Outputs:
- grid_out: bfloat16 [16384, 512], P(('lat', 'lon'))
- weight_grad: bfloat16 [4, 3, 512, 512], replicated
- gain_grad: float32 [4, 512], replicated
Inputs may be any that keep to these rules, and one draw needn't show every extreme that they name: `encode_senders`: on every device each of the 128 received slots is named by some edge of the first 4 blocks. `encode_receivers`: on every device each of its 128 mesh rows is named by some edge of the first 4 blocks. `encode_blocks`: some device has 12 live blocks. `process_senders`: on every device each of the 128 received slots is named by some edge of the first 4 blocks. `process_receivers`: on every device each of its 128 mesh rows is named by some edge of the first 4 blocks. `process_blocks`: some device has 12 live blocks. `decode_senders`: on every device each of the 128 received slots is named by some edge of the first 4 blocks. `decode_receivers`: on every device each of its 512 grid rows is named by some edge of the first 4 blocks. `decode_blocks`: some device has 12 live blocks.
All inputs are finite; a program needn't handle non-finite values.
Results may differ from a plain program's by a relative error of at most 0.017.
Values may be sent and summed in bfloat16 or wider, within the bound.
No kernel may reach another device: no remote copies, remote signals or barrier semaphores. Data moves between devices by JAX's collectives and lax.ppermute only.
A program may use at most 128 MiB of HBM per device.

v0:
```python
import jax
import jax.numpy as jnp
from jax import lax
from jax.sharding import PartitionSpec as P

LAYERS = 2
EDGE_BLOCK = 128
EPSILON = 1e-05


def silu_slope(values):
    sigma = jax.nn.sigmoid(values)
    return sigma * (1.0 + values * (1.0 - sigma))


def transposed_product(left, right):
    return lax.dot_general(
        left, right, (((0,), (0,)), ((), ())), preferred_element_type=jnp.float32
    )


def back_product(grad, weight):
    return lax.dot_general(
        grad, weight, (((1,), (1,)), ((), ())), preferred_element_type=jnp.float32
    )


def projected(latent, weight):
    return jnp.dot(latent, weight, preferred_element_type=jnp.float32).astype(jnp.bfloat16)


def edge_forward(
    slot_vals, proj_recv, latent_recv, senders, receivers, live_mask, weight_out, block_gain
):
    preact = slot_vals[senders].astype(jnp.float32) + proj_recv[receivers].astype(jnp.float32)
    hidden = jax.nn.silu(preact) * live_mask[:, None]
    summed = jax.ops.segment_sum(hidden, receivers, num_segments=proj_recv.shape[0]).astype(
        jnp.bfloat16
    )
    mixed = jnp.dot(summed, weight_out, preferred_element_type=jnp.float32)
    centred = mixed - jnp.mean(mixed, axis=-1, keepdims=True)
    inv_scale = lax.rsqrt(jnp.mean(centred * centred, axis=-1, keepdims=True) + EPSILON)
    normed = centred * inv_scale
    output = (latent_recv.astype(jnp.float32) + normed * block_gain).astype(jnp.bfloat16)
    return (output, preact, summed, normed, inv_scale)


def edge_backward(
    grad_out,
    preact,
    summed,
    normed,
    inv_scale,
    senders,
    receivers,
    live_mask,
    weight_out,
    block_gain,
    recv_count,
    slot_count,
):
    gain_part = jnp.sum(grad_out * normed, axis=0)
    grad_normed = grad_out * block_gain
    grad_mixed = inv_scale * (
        grad_normed
        - jnp.mean(grad_normed, axis=-1, keepdims=True)
        - normed * jnp.mean(grad_normed * normed, axis=-1, keepdims=True)
    )
    grad_mixed = grad_mixed.astype(jnp.bfloat16)
    out_part = transposed_product(summed, grad_mixed)
    grad_summed = back_product(grad_mixed, weight_out)
    grad_pre = grad_summed[receivers] * live_mask[:, None] * silu_slope(preact)
    grad_recv = jax.ops.segment_sum(grad_pre, receivers, num_segments=recv_count).astype(
        jnp.bfloat16
    )
    grad_slots = jax.ops.segment_sum(grad_pre, senders, num_segments=slot_count).astype(
        jnp.bfloat16
    )
    return (grad_recv, grad_slots, out_part, gain_part)


def trade(buffer):
    return lax.all_to_all(buffer, ("lat", "lon"), split_axis=0, concat_axis=0, tiled=True)


def graph_parts(send_rows, senders, receivers, block_count):
    positions = jnp.arange(senders.shape[1], dtype=jnp.int32) // EDGE_BLOCK
    live_mask = (positions < block_count[0]).astype(jnp.float32)
    return (send_rows[0], senders[0], receivers[0], live_mask)


def run_forward(latent_send, latent_recv, weights, block_gain, graph):
    send_rows, senders, receivers, live_mask = graph
    proj_send = projected(latent_send, weights[0])
    outgoing = proj_send[send_rows]
    proj_recv = projected(latent_recv, weights[1])
    slot_vals = trade(outgoing).reshape(-1, proj_send.shape[1])
    output, preact, summed, normed, inv_scale = edge_forward(
        slot_vals, proj_recv, latent_recv, senders, receivers, live_mask, weights[2], block_gain
    )
    return (output, (preact, summed, normed, inv_scale, slot_vals.shape[0]))


def run_backward(grad_out, latent_send, latent_recv, weights, block_gain, graph, saved):
    send_rows, senders, receivers, live_mask = graph
    preact, summed, normed, inv_scale, slot_count = saved
    grad_recv, grad_slots, out_part, gain_part = edge_backward(
        grad_out,
        preact,
        summed,
        normed,
        inv_scale,
        senders,
        receivers,
        live_mask,
        weights[2],
        block_gain,
        latent_recv.shape[0],
        slot_count,
    )
    width = grad_slots.shape[1]
    returned = trade(grad_slots.reshape(send_rows.shape + (width,)))
    grad_send = (
        jnp.zeros((latent_send.shape[0], width), jnp.float32)
        .at[send_rows.reshape(-1)]
        .add(returned.reshape(-1, width).astype(jnp.float32))
        .astype(jnp.bfloat16)
    )
    grad_weights = jnp.stack(
        [
            transposed_product(latent_send, grad_send),
            transposed_product(latent_recv, grad_recv),
            out_part,
        ]
    )
    return (grad_weights, gain_part, grad_send, grad_recv)


def settle(grad_weights, gain_part):
    return (grad_weights, gain_part)


def shards(
    grid_latent,
    mesh_latent,
    block_weights,
    block_gains,
    grid_cot,
    encode_rows,
    encode_senders,
    encode_receivers,
    encode_blocks,
    process_rows,
    process_senders,
    process_receivers,
    process_blocks,
    decode_rows,
    decode_senders,
    decode_receivers,
    decode_blocks,
):
    encode = graph_parts(encode_rows, encode_senders, encode_receivers, encode_blocks)
    process = graph_parts(process_rows, process_senders, process_receivers, process_blocks)
    decode = graph_parts(decode_rows, decode_senders, decode_receivers, decode_blocks)
    latents = [mesh_latent]
    saves = []
    output, saved = run_forward(grid_latent, mesh_latent, block_weights[0], block_gains[0], encode)
    latents.append(output)
    saves.append(saved)
    for layer_id in range(LAYERS):
        current = latents[-1]
        output, saved = run_forward(
            current, current, block_weights[layer_id + 1], block_gains[layer_id + 1], process
        )
        latents.append(output)
        saves.append(saved)
    last_id = LAYERS + 1
    grid_out, decode_saved = run_forward(
        latents[-1], grid_latent, block_weights[last_id], block_gains[last_id], decode
    )
    weight_parts = [None] * (LAYERS + 2)
    gain_parts = [None] * (LAYERS + 2)
    grad_weights, gain_part, grad_send, grad_recv = run_backward(
        grid_cot.astype(jnp.float32),
        latents[-1],
        grid_latent,
        block_weights[last_id],
        block_gains[last_id],
        decode,
        decode_saved,
    )
    weight_parts[last_id], gain_parts[last_id] = settle(grad_weights, gain_part)
    grad_mesh = back_product(grad_send, block_weights[last_id][0])
    for layer_id in reversed(range(LAYERS)):
        block_id = layer_id + 1
        current = latents[block_id]
        grad_weights, gain_part, grad_send, grad_recv = run_backward(
            grad_mesh,
            current,
            current,
            block_weights[block_id],
            block_gains[block_id],
            process,
            saves[block_id],
        )
        weight_parts[block_id], gain_parts[block_id] = settle(grad_weights, gain_part)
        grad_mesh = (
            grad_mesh
            + back_product(grad_recv, block_weights[block_id][1])
            + back_product(grad_send, block_weights[block_id][0])
        )
    grad_weights, gain_part, grad_send, grad_recv = run_backward(
        grad_mesh, grid_latent, mesh_latent, block_weights[0], block_gains[0], encode, saves[0]
    )
    weight_parts[0], gain_parts[0] = settle(grad_weights, gain_part)
    weight_stack = jnp.stack(weight_parts)
    gain_stack = jnp.stack(gain_parts)
    weight_stack, gain_stack = lax.psum((weight_stack, gain_stack), ("lat", "lon"))
    return (grid_out, weight_stack.astype(jnp.bfloat16), gain_stack)


def solution(mesh):
    return jax.shard_map(
        shards,
        mesh=mesh,
        in_specs=(
            P(("lat", "lon"), None),
            P(("lat", "lon"), None),
            P(),
            P(),
            P(("lat", "lon"), None),
            P(("lat", "lon"), None, None),
            P(("lat", "lon"), None),
            P(("lat", "lon"), None),
            P(("lat", "lon")),
            P(("lat", "lon"), None, None),
            P(("lat", "lon"), None),
            P(("lat", "lon"), None),
            P(("lat", "lon")),
            P(("lat", "lon"), None, None),
            P(("lat", "lon"), None),
            P(("lat", "lon"), None),
            P(("lat", "lon")),
        ),
        out_specs=(P(("lat", "lon"), None), P(), P()),
        check_vma=False,
    )
```

profile of v0, /device:TPU:0, one launch (start us, length us, event | category | flops | bytes accessed | tf_op | source)
XLA Modules:
  0.0 602.4 jit_solution(12311952505016923633)
XLA Ops:
  1.7 1.6 convolution_convert_fusion.1
  4.9 7.3 %all-to-all-start = ((bf16[32,4,512]{2,1,0:T(4,128)(2,1)}), bf16[32,4,512]{2,1,0:T(4,128)(2,1)S(1)}, u32[]{:S(2)}, u32[]{:S(2)}) async-start(bf16[32,4,512]{2,1,0:T(4,128)(2,1)} %reshape.518), calls=%async_computation | async-start | bytes 262144 | tf_op jit(solution)/shard_map/all_to_all | solution.py:83
  19.4 4.8 gather_fusion.2
  24.2 1.5 convolution_convert_fusion
  25.8 5.4 gather_fusion.1
  31.2 11.8 %scatter_custom_fusion = f32[128,512]{1,0:T(8,128)S(1)} fusion(s32[1536]{0:T(1024)S(1)} %reduce.1, bf16[1536,512]{1,0:T(8,128)(2,1)S(1)} %gather_fusion.2, bf16[1536,512]{1,0:T(8,128)(2,1)} %gather_fusion.1, f32[1536]{0:T(1024)S(1)} %fusion.133, f32[]{:T(128)} %constant.63.clone.1, f32[]{:T(128)} %constant.59.clone.1), kind=kCustom, calls=%fused_computation.56 | custom fusion | flops 7077888 | bytes 3416072 | tf_op jit(solution)/shard_map/scatter-add | solution.py:37
  43.0 1.4 fusion.147
  48.3 5.8 all-to-all-start.1
  56.2 5.4 gather_fusion.5
  62.3 5.4 gather_fusion.4
  67.8 11.9 %scatter_custom_fusion.1 = f32[128,512]{1,0:T(8,128)S(1)} fusion(s32[1536]{0:T(1024)S(1)} %reduce.4, bf16[1536,512]{1,0:T(8,128)(2,1)} %gather_fusion.5, bf16[1536,512]{1,0:T(8,128)(2,1)} %gather_fusion.4, f32[1536]{0:T(1024)S(1)} %fusion.134, f32[]{:T(128)} %constant.63.clone.1, f32[]{:T(128)} %constant.59.clone.1), kind=kCustom, calls=%fused_computation.51 | custom fusion | flops 7077888 | bytes 3416072 | tf_op jit(solution)/shard_map/scatter-add | solution.py:37
  79.7 1.4 fusion.148
  85.0 5.2 all-to-all-start.2
  92.0 5.4 gather_fusion.8
  98.4 5.4 gather_fusion.7
  103.8 11.7 %scatter_custom_fusion.2 = f32[128,512]{1,0:T(8,128)S(1)} fusion(s32[1536]{0:T(1024)S(1)} %reduce.4, bf16[1536,512]{1,0:T(8,128)(2,1)} %gather_fusion.8, bf16[1536,512]{1,0:T(8,128)(2,1)} %gather_fusion.7, f32[1536]{0:T(1024)S(1)} %fusion.134, f32[]{:T(128)} %constant.63.clone.1, f32[]{:T(128)} %constant.59.clone.1), kind=kCustom, calls=%fused_computation.46 | custom fusion | flops 7077888 | bytes 3416072 | tf_op jit(solution)/shard_map/scatter-add | solution.py:37
  115.5 1.4 fusion.149
  121.4 4.9 all-to-all-start.3
  134.2 2.1 copy.45
  136.2 5.4 gather_fusion.11
  142.3 5.7 gather_fusion.10
  148.0 13.0 %scatter_custom_fusion.3 = f32[512,512]{1,0:T(8,128)} fusion(s32[1536]{0:T(1024)} %reduce, bf16[1536,512]{1,0:T(8,128)(2,1)S(1)} %copy-done.3, bf16[1536,512]{1,0:T(8,128)(2,1)} %gather_fusion.10, f32[1536]{0:T(1024)} %fusion.135, f32[]{:T(128)} %constant.63.clone.1, f32[]{:T(128)} %constant.59.clone.1), kind=kCustom, calls=%fused_computation.41 | custom fusion | flops 7077888 | bytes 4203520 | tf_op jit(solution)/shard_map/scatter-add | solution.py:37
  161.0 1.9 fusion.150
  165.5 1.7 fusion.28
  167.2 4.9 gather_fusion.12
  172.2 4.9 multiply_multiply_fusion.3
  177.0 11.0 %scatter_custom_fusion.4 = f32[128,512]{1,0:T(8,128)} fusion(s32[1536]{0:T(1024)} %reduce.10, f32[1536,512]{1,0:T(8,128)} %multiply_multiply_fusion.3, f32[]{:T(128)} %constant.59.clone.1), kind=kCustom, calls=%fused_computation.206 | custom fusion | flops 786432 | bytes 262656 | tf_op jit(solution)/shard_map/scatter-add | solution.py:76
  189.7 5.8 all-to-all-start.4
  195.5 2.6 convolution_bitcast_fusion
  198.1 10.5 %scatter_custom_fusion.15 = f32[512,512]{1,0:T(8,128)S(1)} fusion(s32[1536]{0:T(1024)} %reduce, f32[1536,512]{1,0:T(8,128)} %multiply_multiply_fusion.3, f32[]{:T(128)} %constant.59.clone.1), kind=kCustom, calls=%fused_computation.141 | custom fusion | flops 786432 | bytes 1049088 | tf_op jit(solution)/shard_map/scatter-add | solution.py:73
  208.6 2.0 copy.56
  210.6 1.5 convolution_bitcast_fusion.1
  212.1 1.8 scatter_custom_fusion.5
  214.0 2.0 multiply_reduce_fusion.1
  220.9 4.9 gather_fusion.13
  225.8 4.5 multiply_multiply_fusion.2
  230.3 10.4 %scatter_custom_fusion.6 = f32[128,512]{1,0:T(8,128)S(1)} fusion(s32[1536]{0:T(1024)} %copy-done.68, f32[1536,512]{1,0:T(8,128)} %multiply_multiply_fusion.2, f32[]{:T(128)} %constant.59.clone.1), kind=kCustom, calls=%fused_computation.202 | custom fusion | flops 786432 | bytes 262656 | tf_op jit(solution)/shard_map/scatter-add | solution.py:73
  240.7 10.3 %scatter_custom_fusion.7 = f32[128,512]{1,0:T(8,128)S(1)} fusion(s32[1536]{0:T(1024)} %reduce.11, f32[1536,512]{1,0:T(8,128)} %multiply_multiply_fusion.2, f32[]{:T(128)} %constant.59.clone.1), kind=kCustom, calls=%fused_computation.200 | custom fusion | flops 786432 | bytes 262656 | tf_op jit(solution)/shard_map/scatter-add | solution.py:76
  251.7 6.0 all-to-all-start.5
  259.0 3.6 maximum_bitcast_fusion.3
  264.0 1.9 all-to-all-done.5
  266.8 1.7 scatter_custom_fusion.8
  268.6 2.1 multiply_reduce_fusion.2
  274.9 4.9 gather_fusion.14
  279.9 4.5 multiply_multiply_fusion.1
  284.4 10.4 %scatter_custom_fusion.9 = f32[128,512]{1,0:T(8,128)S(1)} fusion(s32[1536]{0:T(1024)} %copy-done.68, f32[1536,512]{1,0:T(8,128)} %multiply_multiply_fusion.1, f32[]{:T(128)} %constant.59.clone.1), kind=kCustom, calls=%fused_computation.196 | custom fusion | flops 786432 | bytes 262656 | tf_op jit(solution)/shard_map/scatter-add | solution.py:73
  294.8 10.3 %scatter_custom_fusion.10 = f32[128,512]{1,0:T(8,128)S(1)} fusion(s32[1536]{0:T(1024)} %reduce.11, f32[1536,512]{1,0:T(8,128)} %multiply_multiply_fusion.1, f32[]{:T(128)} %constant.59.clone.1), kind=kCustom, calls=%fused_computation.194 | custom fusion | flops 786432 | bytes 262656 | tf_op jit(solution)/shard_map/scatter-add | solution.py:76
  305.9 4.0 all-to-all-start.6
  311.3 3.6 maximum_bitcast_fusion.2
  316.2 1.8 all-to-all-done.6
  319.0 1.8 scatter_custom_fusion.11
  320.8 2.0 multiply_reduce_fusion.3
  327.1 4.9 gather_fusion.15
  332.1 4.4 multiply_multiply_fusion
  336.4 10.5 %scatter_custom_fusion.14 = f32[128,512]{1,0:T(8,128)S(1)} fusion(s32[1536]{0:T(1024)} %copy-done.67, f32[1536,512]{1,0:T(8,128)} %multiply_multiply_fusion, f32[]{:T(128)} %constant.59.clone.1), kind=kCustom, calls=%fused_computation.188 | custom fusion | flops 786432 | bytes 262656 | tf_op jit(solution)/shard_map/scatter-add | solution.py:73
  346.9 10.3 %scatter_custom_fusion.12 = f32[128,512]{1,0:T(8,128)S(1)} fusion(s32[1536]{0:T(1024)} %reduce.9, f32[1536,512]{1,0:T(8,128)} %multiply_multiply_fusion, f32[]{:T(128)} %constant.59.clone.1), kind=kCustom, calls=%fused_computation.190 | custom fusion | flops 786432 | bytes 262656 | tf_op jit(solution)/shard_map/scatter-add | solution.py:76
  357.9 3.9 all-to-all-start.7
  363.9 3.3 maximum_bitcast_fusion.1
  367.3 2.8 all-to-all-done.7
  370.1 1.7 scatter_custom_fusion.13
  373.4 1.6 copy-done.4
  375.9 6.6 %pad_maximum_fusion = f32[4,3,512,512]{2,3,1,0:T(8,128)} fusion(f32[1,3,512,512]{2,3,1,0:T(8,128)S(1)} %copy-done.4, f32[1,3,512,512]{2,3,1,0:T(8,128)S(1)} %copy-done.5, f32[1,3,512,512]{2,3,1,0:T(8,128)} %maximum_bitcast_fusion.1, f32[1,3,512,512]{2,3,1,0:T(8,128)S(1)} %maximum_bitcast_fusion), kind=kLoop, calls=%fused_computation.32 | loop fusion | flops 9437184 | bytes 25165824 | tf_op jit(solution)/shard_map/stack | solution.py:216
  382.5 210.8 %all-reduce.2 = (bf16[4,3,512,512]{2,3,1,0:T(8,128)(2,1)}, f32[4,512]{1,0:T(4,128)}) all-reduce(f32[4,3,512,512]{2,3,1,0:T(8,128)} %pad_maximum_fusion, f32[4,512]{1,0:T(4,128)S(1)} %pad_maximum_fusion.1), channel_id=1, replica_groups=mesh['lat'=4,'lon'=8] {'lat','lon'}, use_global_device_ids=true, to_apply=%region_32.33 | all-reduce | flops 3147776 | bytes 18890752 | tf_op jit(solution)/shard_map/psum | solution.py:218
  593.3 8.6 %copy.57 = bf16[4,3,512,512]{3,2,1,0:T(8,128)(2,1)} copy(bf16[4,3,512,512]{2,3,1,0:T(8,128)(2,1)} %get-tuple-element.21) | data formatting | bytes 12582912
  (278 shorter events, 64.9 us)
Async XLA Ops:
  0.6 11.6 %copy-start.63 = (s32[1,32,4]{1,2,0:T(4,128)S(1)}, s32[1,32,4]{1,2,0:T(4,128)}, u32[]{:S(2)}) copy-start(s32[1,32,4]{1,2,0:T(4,128)} %param.22) | copy-start | bytes 1540
  0.6 11.7 %copy-start.64 = (s32[1,32,4]{1,2,0:T(4,128)S(1)}, s32[1,32,4]{1,2,0:T(4,128)}, u32[]{:S(2)}) copy-start(s32[1,32,4]{1,2,0:T(4,128)} %param.26) | copy-start | bytes 1540
  0.7 13.7 %copy-start.65 = (s32[1,32,4]{1,2,0:T(4,128)S(1)}, s32[1,32,4]{1,2,0:T(4,128)}, u32[]{:S(2)}) copy-start(s32[1,32,4]{1,2,0:T(4,128)} %param.30) | copy-start | bytes 1540
  0.7 14.4 %copy-start.53 = (s32[1,1536]{1,0:T(1,128)S(1)}, s32[1,1536]{1,0:T(1,128)}, u32[]{:S(2)}) copy-start(s32[1,1536]{1,0:T(1,128)} %param.24) | copy-start | bytes 18436
  0.7 14.4 %copy-start.57 = (s32[1,1536]{1,0:T(1,128)S(1)}, s32[1,1536]{1,0:T(1,128)}, u32[]{:S(2)}) copy-start(s32[1,1536]{1,0:T(1,128)} %param.23) | copy-start | bytes 18436
  0.7 14.5 %copy-start.55 = (s32[1,1536]{1,0:T(1,128)S(1)}, s32[1,1536]{1,0:T(1,128)}, u32[]{:S(2)}) copy-start(s32[1,1536]{1,0:T(1,128)} %param.27) | copy-start | bytes 18436
  0.7 14.5 %copy-start.54 = (s32[1,1536]{1,0:T(1,128)S(1)}, s32[1,1536]{1,0:T(1,128)}, u32[]{:S(2)}) copy-start(s32[1,1536]{1,0:T(1,128)} %param.28) | copy-start | bytes 18436
  0.7 14.6 %copy-start.58 = (s32[1,1536]{1,0:T(1,128)S(1)}, s32[1,1536]{1,0:T(1,128)}, u32[]{:S(2)}) copy-start(s32[1,1536]{1,0:T(1,128)} %param.31) | copy-start | bytes 18436
  0.7 14.6 %copy-start.56 = (s32[1,1536]{1,0:T(1,128)S(1)}, s32[1,1536]{1,0:T(1,128)}, u32[]{:S(2)}) copy-start(s32[1,1536]{1,0:T(1,128)} %param.32) | copy-start | bytes 18436
  0.7 15.2 %copy-start.66 = (f32[4,512]{1,0:T(4,128)S(1)}, f32[4,512]{1,0:T(4,128)}, u32[]{:S(2)}) copy-start(f32[4,512]{1,0:T(4,128)} %param.20) | copy-start | bytes 24580
  0.7 17.4 %copy-start.37 = (bf16[128,512]{1,0:T(8,128)(2,1)S(1)}, bf16[128,512]{1,0:T(8,128)(2,1)}, u32[]{:S(2)}) copy-start(bf16[128,512]{1,0:T(8,128)(2,1)} %param.18) | copy-start | bytes 393220
  4.9 20.8 %all-to-all-start = ((bf16[32,4,512]{2,1,0:T(4,128)(2,1)}), bf16[32,4,512]{2,1,0:T(4,128)(2,1)S(1)}, u32[]{:S(2)}, u32[]{:S(2)}) async-start(bf16[32,4,512]{2,1,0:T(4,128)(2,1)} %reshape.518), calls=%async_computation | async-start | bytes 262144 | tf_op jit(solution)/shard_map/all_to_all | solution.py:83
  14.4 16.8 %copy-start.41 = (f32[1536]{0:T(1024)}, f32[1536]{0:T(1024)S(1)}, u32[]{:S(2)}) copy-start(f32[1536]{0:T(1024)S(1)} %fusion.133) | copy-start | bytes 18436
  15.1 16.1 %copy-start.67 = (s32[1536]{0:T(1024)}, s32[1536]{0:T(1024)S(1)}, u32[]{:S(2)}) copy-start(s32[1536]{0:T(1024)S(1)} %reduce.1) | copy-start | bytes 18436
  15.2 9.0 %copy-start.44 = (s32[2048]{0:T(1024)}, s32[2048]{0:T(1024)S(1)}, u32[]{:S(2)}) copy-start(s32[2048]{0:T(1024)S(1)} %pad_clamp_fusion.4) | copy-start | bytes 24580
  16.6 28.1 %copy-start.48 = (f32[1,512]{1,0:T(1,128)}, f32[1,512]{1,0:T(1,128)S(1)}, u32[]{:S(2)}) copy-start(f32[1,512]{1,0:T(1,128)S(1)} %get-tuple-element.27) | copy-start | bytes 6148
  16.6 64.8 %copy-start.50 = (f32[1,512]{1,0:T(1,128)}, f32[1,512]{1,0:T(1,128)S(1)}, u32[]{:S(2)}) copy-start(f32[1,512]{1,0:T(1,128)S(1)} %get-tuple-element.26) | copy-start | bytes 6148
  43.0 18.7 %copy-start.26 = (f32[128,512]{1,0:T(8,128)}, f32[128,512]{1,0:T(8,128)S(1)}, u32[]{:S(2)}) copy-start(f32[128,512]{1,0:T(8,128)S(1)} %scatter_custom_fusion) | copy-start | bytes 786436
  45.4 36.0 %copy-start.33 = (bf16[128,512]{1,0:T(8,128)(2,1)}, bf16[128,512]{1,0:T(8,128)(2,1)S(1)}, u32[]{:S(2)}) copy-start(bf16[128,512]{1,0:T(8,128)(2,1)S(1)} %add_convert_fusion.3) | copy-start | bytes 393220
  48.3 14.0 %all-to-all-start.1 = ((bf16[32,4,512]{2,1,0:T(4,128)(2,1)}), bf16[32,4,512]{2,1,0:T(4,128)(2,1)S(1)}, u32[]{:S(2)}, u32[]{:S(2)}) async-start(bf16[32,4,512]{2,1,0:T(4,128)(2,1)} %reshape.542), calls=%async_computation.1 | async-start | bytes 262144 | tf_op jit(solution)/shard_map/all_to_all | solution.py:83
  54.7 49.1 %copy-start.68 = (s32[1536]{0:T(1024)}, s32[1536]{0:T(1024)S(1)}, u32[]{:S(2)}) copy-start(s32[1536]{0:T(1024)S(1)} %reduce.4) | copy-start | bytes 18436
  79.7 17.8 %copy-start.28 = (f32[128,512]{1,0:T(8,128)}, f32[128,512]{1,0:T(8,128)S(1)}, u32[]{:S(2)}) copy-start(f32[128,512]{1,0:T(8,128)S(1)} %scatter_custom_fusion.1) | copy-start | bytes 786436
  81.1 16.3 %copy-start.71 = (f32[128]{0:T(128)}, f32[128]{0:T(128)S(1)}, u32[]{:S(2)}) copy-start(f32[128]{0:T(128)S(1)} %broadcast_multiply_fusion.10) | copy-start | bytes 1540
  82.1 35.1 %copy-start.35 = (bf16[128,512]{1,0:T(8,128)(2,1)}, bf16[128,512]{1,0:T(8,128)(2,1)S(1)}, u32[]{:S(2)}) copy-start(bf16[128,512]{1,0:T(8,128)(2,1)S(1)} %add_convert_fusion.2) | copy-start | bytes 393220
  85.0 13.4 %all-to-all-start.2 = ((bf16[32,4,512]{2,1,0:T(4,128)(2,1)}), bf16[32,4,512]{2,1,0:T(4,128)(2,1)S(1)}, u32[]{:S(2)}, u32[]{:S(2)}) async-start(bf16[32,4,512]{2,1,0:T(4,128)(2,1)} %reshape.566), calls=%async_computation.2 | async-start | bytes 262144 | tf_op jit(solution)/shard_map/all_to_all | solution.py:83
  103.8 13.9 %copy-start.52 = (f32[1,512]{1,0:T(1,128)S(1)}, f32[1,512]{1,0:T(1,128)}, u32[]{:S(2)}) copy-start(f32[1,512]{1,0:T(1,128)} %get-tuple-element.28) | copy-start | bytes 6148
  115.5 20.7 %copy-start.30 = (f32[128,512]{1,0:T(8,128)}, f32[128,512]{1,0:T(8,128)S(1)}, u32[]{:S(2)}) copy-start(f32[128,512]{1,0:T(8,128)S(1)} %scatter_custom_fusion.2) | copy-start | bytes 786436
  121.4 20.8 %all-to-all-start.3 = ((bf16[32,4,512]{2,1,0:T(4,128)(2,1)}), bf16[32,4,512]{2,1,0:T(4,128)(2,1)S(1)}, u32[]{:S(2)}, u32[]{:S(2)}) async-start(bf16[32,4,512]{2,1,0:T(4,128)(2,1)} %reshape.590), calls=%async_computation.3 | async-start | bytes 262144 | tf_op jit(solution)/shard_map/all_to_all | solution.py:83
  127.1 14.6 %copy-start.46 = (s32[2048]{0:T(1024)}, s32[2048]{0:T(1024)S(1)}, u32[]{:S(2)}) copy-start(s32[2048]{0:T(1024)S(1)} %pad_clamp_fusion) | copy-start | bytes 24580
  142.3 5.7 copy-start.3
  148.0 15.2 %copy-start.59 = (f32[1,512]{1,0:T(1,128)S(1)}, f32[1,512]{1,0:T(1,128)}, u32[]{:S(2)}) copy-start(f32[1,512]{1,0:T(1,128)} %get-tuple-element.25) | copy-start | bytes 6148
  165.5 6.7 %copy-start.15 = (bf16[512,512]{0,1:T(8,128)(2,1)}, bf16[512,512]{0,1:T(8,128)(2,1)S(1)}, u32[]{:S(2)}) copy-start(bf16[512,512]{0,1:T(8,128)(2,1)S(1)} %get-tuple-element.23) | copy-start | bytes 1572868
  172.2 23.3 %copy-start.6 = (f32[512,512]{1,0:T(8,128)S(1)}, f32[512,512]{1,0:T(8,128)}, u32[]{:S(2)}) copy-start(f32[512,512]{1,0:T(8,128)} %scatter_custom_fusion.3) | copy-start | bytes 3145732
  177.0 33.6 %copy-start.12 = (bf16[512,512]{1,0:T(8,128)(2,1)S(1)}, bf16[512,512]{1,0:T(8,128)(2,1)}, u32[]{:S(2)}) copy-start(bf16[512,512]{1,0:T(8,128)(2,1)} %param.17) | copy-start | bytes 1572868
  189.7 22.5 %all-to-all-start.4 = ((bf16[32,4,512]{2,1,0:T(4,128)(2,1)}), bf16[32,4,512]{2,1,0:T(4,128)(2,1)S(1)}, u32[]{:S(2)}, u32[]{:S(2)}) async-start(bf16[32,4,512]{2,1,0:T(4,128)(2,1)} %reshape.509), calls=%async_computation.4 | async-start | bytes 262144 | tf_op jit(solution)/shard_map/all_to_all | solution.py:83
  212.1 6.0 %copy-start.31 = (f32[128,512]{1,0:T(8,128)S(1)}, f32[128,512]{1,0:T(8,128)}, u32[]{:S(2)}) copy-start(f32[128,512]{1,0:T(8,128)} %copy-done.30) | copy-start | bytes 786436
  212.1 7.4 %copy-start.40 = (bf16[128,512]{1,0:T(8,128)(2,1)S(1)}, bf16[128,512]{1,0:T(8,128)(2,1)}, u32[]{:S(2)}) copy-start(bf16[128,512]{1,0:T(8,128)(2,1)} %copy-done.39) | copy-start | bytes 393220
  225.8 31.9 %copy-start.36 = (bf16[128,512]{1,0:T(8,128)(2,1)S(1)}, bf16[128,512]{1,0:T(8,128)(2,1)}, u32[]{:S(2)}) copy-start(bf16[128,512]{1,0:T(8,128)(2,1)} %copy-done.35) | copy-start | bytes 393220
  230.3 28.7 %copy-start.19 = (f32[1,512,512]{1,2,0:T(8,128)S(1)}, f32[1,512,512]{1,2,0:T(8,128)}, u32[]{:S(2)}) copy-start(f32[1,512,512]{1,2,0:T(8,128)} %convolution_bitcast_fusion) | copy-start | bytes 3145732
  251.7 14.1 %all-to-all-start.5 = ((bf16[32,4,512]{2,1,0:T(4,128)(2,1)}), bf16[32,4,512]{2,1,0:T(4,128)(2,1)}, u32[]{:S(2)}, u32[]{:S(2)}) async-start(bf16[32,4,512]{2,1,0:T(4,128)(2,1)} %reshape.510), calls=%async_computation.5 | async-start | bytes 262144 | tf_op jit(solution)/shard_map/all_to_all | solution.py:83
  259.0 9.5 %copy-start.10 = (f32[128,512]{1,0:T(8,128)S(1)}, f32[128,512]{1,0:T(8,128)}, u32[]{:S(2)}) copy-start(f32[128,512]{1,0:T(8,128)} %copy-done.9) | copy-start | bytes 786436
  262.6 8.0 %copy-start.51 = (f32[1,512]{1,0:T(1,128)S(1)}, f32[1,512]{1,0:T(1,128)}, u32[]{:S(2)}) copy-start(f32[1,512]{1,0:T(1,128)} %copy-done.50) | copy-start | bytes 6148
  262.6 8.0 %copy-start.72 = (f32[128]{0:T(128)S(1)}, f32[128]{0:T(128)}, u32[]{:S(2)}) copy-start(f32[128]{0:T(128)} %copy-done.71) | copy-start | bytes 1540
  262.6 8.0 %copy-start.77 = (f32[128]{0:T(128)S(1)}, f32[128]{0:T(128)}, u32[]{:S(2)}) copy-start(f32[128]{0:T(128)} %copy-done.76) | copy-start | bytes 1540
  262.6 9.5 %copy-start.29 = (f32[128,512]{1,0:T(8,128)S(1)}, f32[128,512]{1,0:T(8,128)}, u32[]{:S(2)}) copy-start(f32[128,512]{1,0:T(8,128)} %copy-done.28) | copy-start | bytes 786436
  279.9 30.0 %copy-start.34 = (bf16[128,512]{1,0:T(8,128)(2,1)S(1)}, bf16[128,512]{1,0:T(8,128)(2,1)}, u32[]{:S(2)}) copy-start(bf16[128,512]{1,0:T(8,128)(2,1)} %copy-done.33) | copy-start | bytes 393220
  284.4 26.8 %copy-start.17 = (f32[1,512,512]{1,2,0:T(8,128)S(1)}, f32[1,512,512]{1,2,0:T(8,128)}, u32[]{:S(2)}) copy-start(f32[1,512,512]{1,2,0:T(8,128)} %convolution_bitcast_fusion.3) | copy-start | bytes 3145732
  305.9 12.2 %all-to-all-start.6 = ((bf16[32,4,512]{2,1,0:T(4,128)(2,1)}), bf16[32,4,512]{2,1,0:T(4,128)(2,1)}, u32[]{:S(2)}, u32[]{:S(2)}) async-start(bf16[32,4,512]{2,1,0:T(4,128)(2,1)} %reshape.511), calls=%async_computation.6 | async-start | bytes 262144 | tf_op jit(solution)/shard_map/all_to_all | solution.py:83
  311.3 9.5 %copy-start.8 = (f32[128,512]{1,0:T(8,128)S(1)}, f32[128,512]{1,0:T(8,128)}, u32[]{:S(2)}) copy-start(f32[128,512]{1,0:T(8,128)} %copy-done.7) | copy-start | bytes 786436
  311.3 9.5 %copy-start.49 = (f32[1,512]{1,0:T(1,128)S(1)}, f32[1,512]{1,0:T(1,128)}, u32[]{:S(2)}) copy-start(f32[1,512]{1,0:T(1,128)} %copy-done.48) | copy-start | bytes 6148
  311.3 9.6 %copy-start.70 = (f32[128]{0:T(128)S(1)}, f32[128]{0:T(128)}, u32[]{:S(2)}) copy-start(f32[128]{0:T(128)} %copy-done.69) | copy-start | bytes 1540
  314.8 8.0 %copy-start.75 = (f32[128]{0:T(128)S(1)}, f32[128]{0:T(128)}, u32[]{:S(2)}) copy-start(f32[128]{0:T(128)} %copy-done.74) | copy-start | bytes 1540
  314.8 9.5 %copy-start.27 = (f32[128,512]{1,0:T(8,128)S(1)}, f32[128,512]{1,0:T(8,128)}, u32[]{:S(2)}) copy-start(f32[128,512]{1,0:T(8,128)} %copy-done.26) | copy-start | bytes 786436
  319.0 8.1 %copy-start.45 = (s32[2048]{0:T(1024)S(1)}, s32[2048]{0:T(1024)}, u32[]{:S(2)}) copy-start(s32[2048]{0:T(1024)} %copy-done.44) | copy-start | bytes 24580
  327.1 5.0 copy-start
  327.1 5.0 copy-start.42
  332.0 29.8 %copy-start.38 = (bf16[128,512]{1,0:T(8,128)(2,1)S(1)}, bf16[128,512]{1,0:T(8,128)(2,1)}, u32[]{:S(2)}) copy-start(bf16[128,512]{1,0:T(8,128)(2,1)} %param.18) | copy-start | bytes 393220
  332.0 31.2 %copy-start.61 = (f32[512]{0:T(512)S(1)}, f32[512]{0:T(512)}, u32[]{:S(2)}) copy-start(f32[512]{0:T(512)} %get-tuple-element.9) | copy-start | bytes 6148
  332.0 31.1 %copy-start.62 = (f32[512]{0:T(512)S(1)}, f32[512]{0:T(512)}, u32[]{:S(2)}) copy-start(f32[512]{0:T(512)} %get-tuple-element.16) | copy-start | bytes 6148
  336.4 27.4 %copy-start.16 = (f32[1,512,512]{1,2,0:T(8,128)S(1)}, f32[1,512,512]{1,2,0:T(8,128)}, u32[]{:S(2)}) copy-start(f32[1,512,512]{1,2,0:T(8,128)} %convolution_bitcast_fusion.6) | copy-start | bytes 3145732
  336.4 27.5 %copy-start.18 = (f32[1,512,512]{1,2,0:T(8,128)S(1)}, f32[1,512,512]{1,2,0:T(8,128)}, u32[]{:S(2)}) copy-start(f32[1,512,512]{1,2,0:T(8,128)} %convolution_bitcast_fusion.7) | copy-start | bytes 3145732
  357.9 12.1 %all-to-all-start.7 = ((bf16[32,4,512]{2,1,0:T(4,128)(2,1)}), bf16[32,4,512]{2,1,0:T(4,128)(2,1)S(1)}, u32[]{:S(2)}, u32[]{:S(2)}) async-start(bf16[32,4,512]{2,1,0:T(4,128)(2,1)} %reshape.512), calls=%async_computation.7 | async-start | bytes 262144 | tf_op jit(solution)/shard_map/all_to_all | solution.py:83
  363.9 7.9 %copy-start.13 = (bf16[512,512]{1,0:T(8,128)(2,1)S(1)}, bf16[512,512]{1,0:T(8,128)(2,1)}, u32[]{:S(2)}) copy-start(bf16[512,512]{1,0:T(8,128)(2,1)} %param.17) | copy-start | bytes 1572868
  367.3 5.0 copy-start.20
  (22 other events, 53.7 us)
where the time goes:
time: 613 us; the launch traced here: 602 us
  blocking collectives  211 us (34%)
  other arithmetic  192 us (31%)
  local copies, waits for them, and re-layouts  95.8 us (16%)
  matrix products  48.4 us (8%)
  starting transfers between devices  43.1 us (7%)
  waiting for transfers between devices  8.05 us (1%)
    psum x1, blocking collectives, shards(): lax.psum((weight_stack, gain_stack), ('lat', 'lon'))  211 us
    scatter-add x4, other arithmetic, edge_forward(): jax.ops.segment_sum(hidden, receivers, num_segments=proj_recv.shape[0])  48.4 us
    all_to_all x8, starting transfers between devices, trade(): lax.all_to_all(buffer, ('lat', 'lon'), split_axis=0, concat_axis=0, tiled...  43.1 us
    scatter-add x4, other arithmetic, edge_backward(): jax.ops.segment_sum(grad_pre, senders, num_segments=slot_count)  41.9 us
    scatter-add x4, other arithmetic, edge_backward(): jax.ops.segment_sum(grad_pre, receivers, num_segments=recv_count)  41.7 us
    gather x4, local copies, waits for them, and re-layouts, edge_forward(): slot_vals[senders].astype(jnp.float32)  22 us
    gather x4, local copies, waits for them, and re-layouts, edge_forward(): proj_recv[receivers].astype(jnp.float32)  21.1 us
    unnamed x163, local copies, waits for them, and re-layouts  20.5 us
  transfers between devices with their start and end apart: 8, of which 5 were waited for; matrix products, arithmetic and copies ran while one was open for 13% of the time, Pallas kernels for 0%

commit v1 on v0

--- a/solution.py
+++ b/solution.py
@@ -215,7 +215,7 @@
     weight_parts[0], gain_parts[0] = settle(grad_weights, gain_part)
     weight_stack = jnp.stack(weight_parts)
     gain_stack = jnp.stack(gain_parts)
-    weight_stack, gain_stack = lax.psum((weight_stack, gain_stack), ("lat", "lon"))
+    weight_stack, gain_stack = lax.psum(lax.psum((weight_stack, gain_stack), "lon"), "lat")
     return (grid_out, weight_stack.astype(jnp.bfloat16), gain_stack)
 
 

time: 613 us -> 1010 us (1.65)
  blocking collectives: 211 us -> 439 us
  waiting for transfers between devices: 8.05 us -> 164 us
  between operations: 4.38 us -> 17.7 us
    psum x1 -> x2, blocking collectives: 211 us -> 439 us  [the longest x1 426 us: shards(): lax.psum(lax.psum((weight_stack, gain_stack), 'lon'), 'lat')]
    psum x0 -> x1, waiting for transfers between devices: none -> 155 us  [shards(): lax.psum((weight_stack, gain_stack), 'lon')]
    unnamed x163 -> x169, local copies, waits for them, and re-layouts: 20.5 us -> 20.5 us
  transfers between devices with their start and end apart: 8 -> 9, of which waited for: 5 -> 6; matrix products, arithmetic and copies ran while one was open for 13% -> 7% of each run, Pallas kernels for 0% -> 0%
where the time goes in v1:
time: 1010 us; the launch traced here: 999 us
  blocking collectives  439 us (43%)
  other arithmetic  191 us (19%)
  waiting for transfers between devices  164 us (16%)
  local copies, waits for them, and re-layouts  95.7 us (9%)
  matrix products  48.4 us (5%)
  starting transfers between devices  43.1 us (4%)
  between operations  17.7 us (2%)
    psum x1, blocking collectives, shards(): lax.psum(lax.psum((weight_stack, gain_stack), 'lon'), 'lat')  426 us
    psum x1, waiting for transfers between devices, shards(): lax.psum((weight_stack, gain_stack), 'lon')  155 us
    scatter-add x4, other arithmetic, edge_forward(): jax.ops.segment_sum(hidden, receivers, num_segments=proj_recv.shape[0])  48.4 us
    all_to_all x8, starting transfers between devices, trade(): lax.all_to_all(buffer, ('lat', 'lon'), split_axis=0, concat_axis=0, tiled...  43.1 us
    scatter-add x4, other arithmetic, edge_backward(): jax.ops.segment_sum(grad_pre, senders, num_segments=slot_count)  41.9 us
    scatter-add x4, other arithmetic, edge_backward(): jax.ops.segment_sum(grad_pre, receivers, num_segments=recv_count)  41.7 us
    gather x4, local copies, waits for them, and re-layouts, edge_forward(): slot_vals[senders].astype(jnp.float32)  22 us
    gather x4, local copies, waits for them, and re-layouts, edge_forward(): proj_recv[receivers].astype(jnp.float32)  21.1 us
  transfers between devices with their start and end apart: 9, of which 6 were waited for; matrix products, arithmetic and copies ran while one was open for 7% of the time, Pallas kernels for 0%

profile of v1, /device:TPU:0, one launch (start us, length us, event | category | flops | bytes accessed | tf_op | source)
XLA Modules:
  0.0 999.0 jit_solution(6283096260542524367)
XLA Ops:
  8.2 1.6 convolution_convert_fusion.1
  11.4 7.3 all-to-all-start
  25.9 4.8 gather_fusion.2
  30.7 1.5 convolution_convert_fusion
  32.3 5.4 gather_fusion.1
  37.7 11.8 %scatter_custom_fusion = f32[128,512]{1,0:T(8,128)S(1)} fusion(s32[1536]{0:T(1024)S(1)} %reduce.1, bf16[1536,512]{1,0:T(8,128)(2,1)S(1)} %gather_fusion.2, bf16[1536,512]{1,0:T(8,128)(2,1)} %gather_fusion.1, f32[1536]{0:T(1024)S(1)} %fusion.133, f32[]{:T(128)} %constant.63.clone.1, f32[]{:T(128)} %constant.59.clone.1), kind=kCustom, calls=%fused_computation.56 | custom fusion | flops 7077888 | bytes 3416072 | tf_op jit(solution)/shard_map/scatter-add | solution.py:37
  49.5 1.4 fusion.147
  54.8 5.8 all-to-all-start.1
  62.7 5.4 gather_fusion.5
  68.9 5.4 gather_fusion.4
  74.3 11.9 %scatter_custom_fusion.1 = f32[128,512]{1,0:T(8,128)S(1)} fusion(s32[1536]{0:T(1024)S(1)} %reduce.4, bf16[1536,512]{1,0:T(8,128)(2,1)} %gather_fusion.5, bf16[1536,512]{1,0:T(8,128)(2,1)} %gather_fusion.4, f32[1536]{0:T(1024)S(1)} %fusion.134, f32[]{:T(128)} %constant.63.clone.1, f32[]{:T(128)} %constant.59.clone.1), kind=kCustom, calls=%fused_computation.51 | custom fusion | flops 7077888 | bytes 3416072 | tf_op jit(solution)/shard_map/scatter-add | solution.py:37
  86.2 1.4 fusion.148
  91.5 5.2 all-to-all-start.2
  98.5 5.4 gather_fusion.8
  104.9 5.4 gather_fusion.7
  110.3 11.7 %scatter_custom_fusion.2 = f32[128,512]{1,0:T(8,128)S(1)} fusion(s32[1536]{0:T(1024)S(1)} %reduce.4, bf16[1536,512]{1,0:T(8,128)(2,1)} %gather_fusion.8, bf16[1536,512]{1,0:T(8,128)(2,1)} %gather_fusion.7, f32[1536]{0:T(1024)S(1)} %fusion.134, f32[]{:T(128)} %constant.63.clone.1, f32[]{:T(128)} %constant.59.clone.1), kind=kCustom, calls=%fused_computation.46 | custom fusion | flops 7077888 | bytes 3416072 | tf_op jit(solution)/shard_map/scatter-add | solution.py:37
  122.0 1.4 fusion.149
  127.9 4.9 all-to-all-start.3
  140.7 2.1 copy.45
  142.7 5.4 gather_fusion.11
  148.8 5.7 gather_fusion.10
  154.5 13.0 %scatter_custom_fusion.3 = f32[512,512]{1,0:T(8,128)} fusion(s32[1536]{0:T(1024)} %reduce, bf16[1536,512]{1,0:T(8,128)(2,1)S(1)} %copy-done.3, bf16[1536,512]{1,0:T(8,128)(2,1)} %gather_fusion.10, f32[1536]{0:T(1024)} %fusion.135, f32[]{:T(128)} %constant.63.clone.1, f32[]{:T(128)} %constant.59.clone.1), kind=kCustom, calls=%fused_computation.41 | custom fusion | flops 7077888 | bytes 4203520 | tf_op jit(solution)/shard_map/scatter-add | solution.py:37
  167.5 1.9 fusion.150
  172.0 1.7 fusion.28
  173.7 4.9 gather_fusion.12
  178.7 4.9 multiply_multiply_fusion.3
  183.5 11.0 %scatter_custom_fusion.4 = f32[128,512]{1,0:T(8,128)} fusion(s32[1536]{0:T(1024)} %reduce.10, f32[1536,512]{1,0:T(8,128)} %multiply_multiply_fusion.3, f32[]{:T(128)} %constant.59.clone.1), kind=kCustom, calls=%fused_computation.206 | custom fusion | flops 786432 | bytes 262656 | tf_op jit(solution)/shard_map/scatter-add | solution.py:76
  196.1 5.8 all-to-all-start.4
  202.0 2.6 convolution_bitcast_fusion
  204.6 10.5 %scatter_custom_fusion.15 = f32[512,512]{1,0:T(8,128)S(1)} fusion(s32[1536]{0:T(1024)} %reduce, f32[1536,512]{1,0:T(8,128)} %multiply_multiply_fusion.3, f32[]{:T(128)} %constant.59.clone.1), kind=kCustom, calls=%fused_computation.141 | custom fusion | flops 786432 | bytes 1049088 | tf_op jit(solution)/shard_map/scatter-add | solution.py:73
  216.5 1.8 scatter_custom_fusion.5
  218.4 2.0 multiply_reduce_fusion.1
  225.3 4.9 gather_fusion.13
  230.2 4.5 multiply_multiply_fusion.2
  234.8 10.4 %scatter_custom_fusion.6 = f32[128,512]{1,0:T(8,128)S(1)} fusion(s32[1536]{0:T(1024)} %copy-done.71, f32[1536,512]{1,0:T(8,128)} %multiply_multiply_fusion.2, f32[]{:T(128)} %constant.59.clone.1), kind=kCustom, calls=%fused_computation.202 | custom fusion | flops 786432 | bytes 262656 | tf_op jit(solution)/shard_map/scatter-add | solution.py:73
  245.2 10.3 %scatter_custom_fusion.7 = f32[128,512]{1,0:T(8,128)S(1)} fusion(s32[1536]{0:T(1024)} %reduce.11, f32[1536,512]{1,0:T(8,128)} %multiply_multiply_fusion.2, f32[]{:T(128)} %constant.59.clone.1), kind=kCustom, calls=%fused_computation.200 | custom fusion | flops 786432 | bytes 262656 | tf_op jit(solution)/shard_map/scatter-add | solution.py:76
  256.2 6.0 all-to-all-start.5
  263.5 3.6 maximum_bitcast_fusion.3
  268.5 1.8 all-to-all-done.5
  271.3 1.7 scatter_custom_fusion.8
  273.0 2.0 multiply_reduce_fusion.2
  279.4 4.9 gather_fusion.14
  284.3 4.5 multiply_multiply_fusion.1
  288.9 10.4 %scatter_custom_fusion.9 = f32[128,512]{1,0:T(8,128)S(1)} fusion(s32[1536]{0:T(1024)} %copy-done.71, f32[1536,512]{1,0:T(8,128)} %multiply_multiply_fusion.1, f32[]{:T(128)} %constant.59.clone.1), kind=kCustom, calls=%fused_computation.196 | custom fusion | flops 786432 | bytes 262656 | tf_op jit(solution)/shard_map/scatter-add | solution.py:73
  299.3 10.3 %scatter_custom_fusion.10 = f32[128,512]{1,0:T(8,128)S(1)} fusion(s32[1536]{0:T(1024)} %reduce.11, f32[1536,512]{1,0:T(8,128)} %multiply_multiply_fusion.1, f32[]{:T(128)} %constant.59.clone.1), kind=kCustom, calls=%fused_computation.194 | custom fusion | flops 786432 | bytes 262656 | tf_op jit(solution)/shard_map/scatter-add | solution.py:76
  310.3 4.1 all-to-all-start.6
  315.7 3.6 maximum_bitcast_fusion.2
  320.7 1.9 all-to-all-done.6
  323.5 1.8 scatter_custom_fusion.11
  325.3 2.0 multiply_reduce_fusion.3
  331.6 4.9 gather_fusion.15
  336.5 4.4 multiply_multiply_fusion
  340.9 10.5 %scatter_custom_fusion.14 = f32[128,512]{1,0:T(8,128)S(1)} fusion(s32[1536]{0:T(1024)} %copy-done.70, f32[1536,512]{1,0:T(8,128)} %multiply_multiply_fusion, f32[]{:T(128)} %constant.59.clone.1), kind=kCustom, calls=%fused_computation.188 | custom fusion | flops 786432 | bytes 262656 | tf_op jit(solution)/shard_map/scatter-add | solution.py:73
  351.4 10.3 %scatter_custom_fusion.12 = f32[128,512]{1,0:T(8,128)S(1)} fusion(s32[1536]{0:T(1024)} %reduce.9, f32[1536,512]{1,0:T(8,128)} %multiply_multiply_fusion, f32[]{:T(128)} %constant.59.clone.1), kind=kCustom, calls=%fused_computation.190 | custom fusion | flops 786432 | bytes 262656 | tf_op jit(solution)/shard_map/scatter-add | solution.py:76
  362.4 3.9 all-to-all-start.7
  367.7 3.4 maximum_bitcast_fusion.1
  371.1 3.4 all-to-all-done.7
  374.6 1.7 scatter_custom_fusion.13
  377.8 1.6 copy-done.4
  380.4 6.7 pad_maximum_fusion
  389.2 13.5 %psum.30 = f32[4,512]{1,0:T(4,128)S(1)} all-reduce(f32[4,512]{1,0:T(4,128)S(1)} %pad_maximum_fusion.1), channel_id=1, replica_groups=mesh['lat'=4,'lon'=8] {'lon'}, use_global_device_ids=true, to_apply=%region_38.39 | all-reduce | flops 2048 | bytes 16384 | tf_op jit(solution)/shard_map/psum | solution.py:218
  402.7 154.9 %all-reduce.4.cloned.1.call-done = f32[4,3,512,512]{2,3,1,0:T(8,128)} async-done(((f32[4,3,512,512]{2,3,1,0:T(8,128)}), f32[4,3,512,512]{2,3,1,0:T(8,128)}) %all-reduce.4.cloned.1.call-update) | async-done | bytes 12582928 | tf_op jit(solution)/shard_map/psum | solution.py:218
  557.6 425.6 %all-reduce.5 = (bf16[4,3,512,512]{2,3,1,0:T(8,128)(2,1)}, f32[4,512]{1,0:T(4,128)}) all-reduce(f32[4,3,512,512]{2,3,1,0:T(8,128)} %all-reduce.4.cloned.1.call-done, f32[4,512]{1,0:T(4,128)S(1)} %psum.30), channel_id=1, replica_groups=mesh['lat'=4,'lon'=8] {'lat'}, use_global_device_ids=true, to_apply=%region_33.34 | all-reduce | flops 3147776 | bytes 18890752 | tf_op jit(solution)/shard_map/psum | solution.py:218
  983.1 8.6 copy.57
  (288 shorter events, 67.8 us)
Async XLA Ops:
  7.2 11.6 %copy-start.66 = (s32[1,32,4]{1,2,0:T(4,128)S(1)}, s32[1,32,4]{1,2,0:T(4,128)}, u32[]{:S(2)}) copy-start(s32[1,32,4]{1,2,0:T(4,128)} %param.22) | copy-start | bytes 1540
  7.2 11.7 %copy-start.67 = (s32[1,32,4]{1,2,0:T(4,128)S(1)}, s32[1,32,4]{1,2,0:T(4,128)}, u32[]{:S(2)}) copy-start(s32[1,32,4]{1,2,0:T(4,128)} %param.26) | copy-start | bytes 1540
  7.2 13.7 %copy-start.68 = (s32[1,32,4]{1,2,0:T(4,128)S(1)}, s32[1,32,4]{1,2,0:T(4,128)}, u32[]{:S(2)}) copy-start(s32[1,32,4]{1,2,0:T(4,128)} %param.30) | copy-start | bytes 1540
  7.2 14.4 %copy-start.54 = (s32[1,1536]{1,0:T(1,128)S(1)}, s32[1,1536]{1,0:T(1,128)}, u32[]{:S(2)}) copy-start(s32[1,1536]{1,0:T(1,128)} %param.24) | copy-start | bytes 18436
  7.2 14.4 %copy-start.58 = (s32[1,1536]{1,0:T(1,128)S(1)}, s32[1,1536]{1,0:T(1,128)}, u32[]{:S(2)}) copy-start(s32[1,1536]{1,0:T(1,128)} %param.23) | copy-start | bytes 18436
  7.2 14.5 %copy-start.56 = (s32[1,1536]{1,0:T(1,128)S(1)}, s32[1,1536]{1,0:T(1,128)}, u32[]{:S(2)}) copy-start(s32[1,1536]{1,0:T(1,128)} %param.27) | copy-start | bytes 18436
  7.2 14.5 %copy-start.55 = (s32[1,1536]{1,0:T(1,128)S(1)}, s32[1,1536]{1,0:T(1,128)}, u32[]{:S(2)}) copy-start(s32[1,1536]{1,0:T(1,128)} %param.28) | copy-start | bytes 18436
  7.2 14.6 %copy-start.59 = (s32[1,1536]{1,0:T(1,128)S(1)}, s32[1,1536]{1,0:T(1,128)}, u32[]{:S(2)}) copy-start(s32[1,1536]{1,0:T(1,128)} %param.31) | copy-start | bytes 18436
  7.3 14.6 %copy-start.57 = (s32[1,1536]{1,0:T(1,128)S(1)}, s32[1,1536]{1,0:T(1,128)}, u32[]{:S(2)}) copy-start(s32[1,1536]{1,0:T(1,128)} %param.32) | copy-start | bytes 18436
  7.3 15.2 %copy-start.69 = (f32[4,512]{1,0:T(4,128)S(1)}, f32[4,512]{1,0:T(4,128)}, u32[]{:S(2)}) copy-start(f32[4,512]{1,0:T(4,128)} %param.20) | copy-start | bytes 24580
  7.3 17.3 %copy-start.38 = (bf16[128,512]{1,0:T(8,128)(2,1)S(1)}, bf16[128,512]{1,0:T(8,128)(2,1)}, u32[]{:S(2)}) copy-start(bf16[128,512]{1,0:T(8,128)(2,1)} %param.18) | copy-start | bytes 393220
  11.4 20.8 %all-to-all-start = ((bf16[32,4,512]{2,1,0:T(4,128)(2,1)}), bf16[32,4,512]{2,1,0:T(4,128)(2,1)S(1)}, u32[]{:S(2)}, u32[]{:S(2)}) async-start(bf16[32,4,512]{2,1,0:T(4,128)(2,1)} %reshape.518), calls=%async_computation | async-start | bytes 262144 | tf_op jit(solution)/shard_map/all_to_all | solution.py:83
  20.9 16.7 %copy-start.42 = (f32[1536]{0:T(1024)}, f32[1536]{0:T(1024)S(1)}, u32[]{:S(2)}) copy-start(f32[1536]{0:T(1024)S(1)} %fusion.133) | copy-start | bytes 18436
  21.6 16.1 %copy-start.70 = (s32[1536]{0:T(1024)}, s32[1536]{0:T(1024)S(1)}, u32[]{:S(2)}) copy-start(s32[1536]{0:T(1024)S(1)} %reduce.1) | copy-start | bytes 18436
  21.7 9.0 copy-start.45
  23.1 28.1 %copy-start.49 = (f32[1,512]{1,0:T(1,128)}, f32[1,512]{1,0:T(1,128)S(1)}, u32[]{:S(2)}) copy-start(f32[1,512]{1,0:T(1,128)S(1)} %get-tuple-element.27) | copy-start | bytes 6148
  23.1 64.8 %copy-start.51 = (f32[1,512]{1,0:T(1,128)}, f32[1,512]{1,0:T(1,128)S(1)}, u32[]{:S(2)}) copy-start(f32[1,512]{1,0:T(1,128)S(1)} %get-tuple-element.26) | copy-start | bytes 6148
  49.5 18.7 %copy-start.26 = (f32[128,512]{1,0:T(8,128)}, f32[128,512]{1,0:T(8,128)S(1)}, u32[]{:S(2)}) copy-start(f32[128,512]{1,0:T(8,128)S(1)} %scatter_custom_fusion) | copy-start | bytes 786436
  51.9 36.0 %copy-start.34 = (bf16[128,512]{1,0:T(8,128)(2,1)}, bf16[128,512]{1,0:T(8,128)(2,1)S(1)}, u32[]{:S(2)}) copy-start(bf16[128,512]{1,0:T(8,128)(2,1)S(1)} %add_convert_fusion.3) | copy-start | bytes 393220
  54.8 14.0 %all-to-all-start.1 = ((bf16[32,4,512]{2,1,0:T(4,128)(2,1)}), bf16[32,4,512]{2,1,0:T(4,128)(2,1)S(1)}, u32[]{:S(2)}, u32[]{:S(2)}) async-start(bf16[32,4,512]{2,1,0:T(4,128)(2,1)} %reshape.542), calls=%async_computation.1 | async-start | bytes 262144 | tf_op jit(solution)/shard_map/all_to_all | solution.py:83
  61.2 49.1 %copy-start.71 = (s32[1536]{0:T(1024)}, s32[1536]{0:T(1024)S(1)}, u32[]{:S(2)}) copy-start(s32[1536]{0:T(1024)S(1)} %reduce.4) | copy-start | bytes 18436
  86.2 17.8 %copy-start.28 = (f32[128,512]{1,0:T(8,128)}, f32[128,512]{1,0:T(8,128)S(1)}, u32[]{:S(2)}) copy-start(f32[128,512]{1,0:T(8,128)S(1)} %scatter_custom_fusion.1) | copy-start | bytes 786436
  87.6 16.3 %copy-start.74 = (f32[128]{0:T(128)}, f32[128]{0:T(128)S(1)}, u32[]{:S(2)}) copy-start(f32[128]{0:T(128)S(1)} %broadcast_multiply_fusion.10) | copy-start | bytes 1540
  88.6 35.1 %copy-start.36 = (bf16[128,512]{1,0:T(8,128)(2,1)}, bf16[128,512]{1,0:T(8,128)(2,1)S(1)}, u32[]{:S(2)}) copy-start(bf16[128,512]{1,0:T(8,128)(2,1)S(1)} %add_convert_fusion.2) | copy-start | bytes 393220
  91.5 13.4 %all-to-all-start.2 = ((bf16[32,4,512]{2,1,0:T(4,128)(2,1)}), bf16[32,4,512]{2,1,0:T(4,128)(2,1)S(1)}, u32[]{:S(2)}, u32[]{:S(2)}) async-start(bf16[32,4,512]{2,1,0:T(4,128)(2,1)} %reshape.566), calls=%async_computation.2 | async-start | bytes 262144 | tf_op jit(solution)/shard_map/all_to_all | solution.py:83
  110.3 13.9 %copy-start.53 = (f32[1,512]{1,0:T(1,128)S(1)}, f32[1,512]{1,0:T(1,128)}, u32[]{:S(2)}) copy-start(f32[1,512]{1,0:T(1,128)} %get-tuple-element.28) | copy-start | bytes 6148
  122.0 20.7 %copy-start.30 = (f32[128,512]{1,0:T(8,128)}, f32[128,512]{1,0:T(8,128)S(1)}, u32[]{:S(2)}) copy-start(f32[128,512]{1,0:T(8,128)S(1)} %scatter_custom_fusion.2) | copy-start | bytes 786436
  127.9 20.8 %all-to-all-start.3 = ((bf16[32,4,512]{2,1,0:T(4,128)(2,1)}), bf16[32,4,512]{2,1,0:T(4,128)(2,1)S(1)}, u32[]{:S(2)}, u32[]{:S(2)}) async-start(bf16[32,4,512]{2,1,0:T(4,128)(2,1)} %reshape.590), calls=%async_computation.3 | async-start | bytes 262144 | tf_op jit(solution)/shard_map/all_to_all | solution.py:83
  133.6 14.6 %copy-start.47 = (s32[2048]{0:T(1024)}, s32[2048]{0:T(1024)S(1)}, u32[]{:S(2)}) copy-start(s32[2048]{0:T(1024)S(1)} %pad_clamp_fusion) | copy-start | bytes 24580
  148.8 5.7 copy-start.3
  154.5 15.2 %copy-start.60 = (f32[1,512]{1,0:T(1,128)S(1)}, f32[1,512]{1,0:T(1,128)}, u32[]{:S(2)}) copy-start(f32[1,512]{1,0:T(1,128)} %get-tuple-element.25) | copy-start | bytes 6148
  172.0 6.7 copy-start.15
  178.7 23.3 %copy-start.6 = (f32[512,512]{1,0:T(8,128)S(1)}, f32[512,512]{1,0:T(8,128)}, u32[]{:S(2)}) copy-start(f32[512,512]{1,0:T(8,128)} %scatter_custom_fusion.3) | copy-start | bytes 3145732
  183.5 31.5 %copy-start.12 = (bf16[512,512]{1,0:T(8,128)(2,1)S(1)}, bf16[512,512]{1,0:T(8,128)(2,1)}, u32[]{:S(2)}) copy-start(bf16[512,512]{1,0:T(8,128)(2,1)} %param.17) | copy-start | bytes 1572868
  196.1 20.4 %all-to-all-start.4 = ((bf16[32,4,512]{2,1,0:T(4,128)(2,1)}), bf16[32,4,512]{2,1,0:T(4,128)(2,1)S(1)}, u32[]{:S(2)}, u32[]{:S(2)}) async-start(bf16[32,4,512]{2,1,0:T(4,128)(2,1)} %reshape.509), calls=%async_computation.4 | async-start | bytes 262144 | tf_op jit(solution)/shard_map/all_to_all | solution.py:83
  216.5 6.1 copy-start.31
  216.5 7.5 copy-start.41
  230.2 31.9 %copy-start.37 = (bf16[128,512]{1,0:T(8,128)(2,1)S(1)}, bf16[128,512]{1,0:T(8,128)(2,1)}, u32[]{:S(2)}) copy-start(bf16[128,512]{1,0:T(8,128)(2,1)} %copy-done.36) | copy-start | bytes 393220
  234.8 28.8 %copy-start.19 = (f32[1,512,512]{1,2,0:T(8,128)S(1)}, f32[1,512,512]{1,2,0:T(8,128)}, u32[]{:S(2)}) copy-start(f32[1,512,512]{1,2,0:T(8,128)} %convolution_bitcast_fusion) | copy-start | bytes 3145732
  256.2 14.1 %all-to-all-start.5 = ((bf16[32,4,512]{2,1,0:T(4,128)(2,1)}), bf16[32,4,512]{2,1,0:T(4,128)(2,1)}, u32[]{:S(2)}, u32[]{:S(2)}) async-start(bf16[32,4,512]{2,1,0:T(4,128)(2,1)} %reshape.510), calls=%async_computation.5 | async-start | bytes 262144 | tf_op jit(solution)/shard_map/all_to_all | solution.py:83
  263.5 9.5 copy-start.10
  267.1 8.0 copy-start.52
  267.1 8.0 copy-start.75
  267.1 8.0 copy-start.80
  267.1 9.5 copy-start.29
  279.4 4.9 copy-start.1
  284.3 30.1 %copy-start.35 = (bf16[128,512]{1,0:T(8,128)(2,1)S(1)}, bf16[128,512]{1,0:T(8,128)(2,1)}, u32[]{:S(2)}) copy-start(bf16[128,512]{1,0:T(8,128)(2,1)} %copy-done.34) | copy-start | bytes 393220
  288.9 26.8 %copy-start.17 = (f32[1,512,512]{1,2,0:T(8,128)S(1)}, f32[1,512,512]{1,2,0:T(8,128)}, u32[]{:S(2)}) copy-start(f32[1,512,512]{1,2,0:T(8,128)} %convolution_bitcast_fusion.3) | copy-start | bytes 3145732
  310.3 12.3 %all-to-all-start.6 = ((bf16[32,4,512]{2,1,0:T(4,128)(2,1)}), bf16[32,4,512]{2,1,0:T(4,128)(2,1)}, u32[]{:S(2)}, u32[]{:S(2)}) async-start(bf16[32,4,512]{2,1,0:T(4,128)(2,1)} %reshape.511), calls=%async_computation.6 | async-start | bytes 262144 | tf_op jit(solution)/shard_map/all_to_all | solution.py:83
  315.7 9.6 copy-start.8
  315.7 9.6 copy-start.50
  315.7 9.6 copy-start.73
  319.3 8.1 copy-start.78
  319.3 9.6 copy-start.27
  323.5 8.1 copy-start.46
  331.6 5.0 copy-start
  331.6 5.0 copy-start.43
  336.5 29.8 %copy-start.39 = (bf16[128,512]{1,0:T(8,128)(2,1)S(1)}, bf16[128,512]{1,0:T(8,128)(2,1)}, u32[]{:S(2)}) copy-start(bf16[128,512]{1,0:T(8,128)(2,1)} %param.18) | copy-start | bytes 393220
  340.9 26.8 %copy-start.16 = (f32[1,512,512]{1,2,0:T(8,128)S(1)}, f32[1,512,512]{1,2,0:T(8,128)}, u32[]{:S(2)}) copy-start(f32[1,512,512]{1,2,0:T(8,128)} %convolution_bitcast_fusion.6) | copy-start | bytes 3145732
  340.9 26.8 %copy-start.18 = (f32[1,512,512]{1,2,0:T(8,128)S(1)}, f32[1,512,512]{1,2,0:T(8,128)}, u32[]{:S(2)}) copy-start(f32[1,512,512]{1,2,0:T(8,128)} %convolution_bitcast_fusion.7) | copy-start | bytes 3145732
  362.4 12.1 %all-to-all-start.7 = ((bf16[32,4,512]{2,1,0:T(4,128)(2,1)}), bf16[32,4,512]{2,1,0:T(4,128)(2,1)S(1)}, u32[]{:S(2)}, u32[]{:S(2)}) async-start(bf16[32,4,512]{2,1,0:T(4,128)(2,1)} %reshape.512), calls=%async_computation.7 | async-start | bytes 262144 | tf_op jit(solution)/shard_map/all_to_all | solution.py:83
  366.3 191.3 %all-reduce.4.cloned.1.call-start = ((), (), s32[]{:S(2)}) async-start(), calls=%async_computation.8 | async-start | bytes 25165824 | tf_op jit(solution)/shard_map/psum | solution.py:218
  367.7 8.6 copy-start.13
  371.1 5.7 copy-start.20
  (26 other events, 58.0 us)
Sparse Core Ops, SparseCore 0:
  387.2 170.2 all-reduce.3
